TPU v7x, 32 devices: a whole 2x2x4 slice. The times are simulated.
32 devices in a mesh: dp: 8 (over y, x, core), tensor: 4 (over z).
Axes of the slice: x: 2, y: 2, z: 4, core: 2. Of those that a mesh axis runs over, the one named last changes fastest.
Arguments:
- inputs: bfloat16 [12288, 768], P(('dp', 'tensor')), may hold values from -6 to 6
- segments: int32 [24, 512], P('dp'), may hold values from 0 to 3, never falling along the last dimension, each value on 1 to 256 neighbouring positions
- labels: int32 [24], P('dp'), may hold values from 0 to 2
- qkv_weight: bfloat16 [3, 768, 768], P(None, None, 'tensor'), may hold values from -0.21875 to 0.21875
- qv_bias: float32 [2, 768], P(None, 'tensor'), may hold values from -3 to 3
- out_weight: bfloat16 [768, 768], P('tensor'), may hold values from -0.875 to 0.875
- out_bias: float32 [768], replicated, may hold values from -3 to 3
- norm1_gain: float32 [768], replicated, may hold values from 0.5 to 1.5
- norm1_bias: float32 [768], replicated, may hold values from -3 to 3
- up_weight: bfloat16 [768, 3072], P(None, 'tensor'), may hold values from -0.21875 to 0.21875
- up_bias: float32 [3072], P('tensor'), may hold values from -3 to 3
- down_weight: bfloat16 [3072, 768], P('tensor'), may hold values from -0.109375 to 0.109375
- down_bias: float32 [768], replicated, may hold values from -3 to 3
- norm2_gain: float32 [768], replicated, may hold values from 0.5 to 1.5
- norm2_bias: float32 [768], replicated, may hold values from -3 to 3
- pool_weight: bfloat16 [768, 768], replicated, may hold values from -0.21875 to 0.21875
- pool_bias: float32 [768], replicated, may hold values from -3 to 3
- class_weight: bfloat16 [768, 3], replicated, may hold values from -0.4375 to 0.4375
- class_bias: float32 [3], replicated, may hold values from -4 to 4
- cotangent: bfloat16 [12288, 768], P(('dp', 'tensor')), may hold values from -6 to 6
Outputs:
- hidden: bfloat16 [12288, 768], P(('dp', 'tensor'))
- input_grad: bfloat16 [12288, 768], P(('dp', 'tensor'))
- qkv_weight_grad: float32 [3, 768, 768], P(None, 'dp', 'tensor')
- qv_bias_grad: float32 [2, 768], P(None, 'tensor')
- out_weight_grad: float32 [768, 768], P('tensor', 'dp')
- out_bias_grad: float32 [768], replicated
- norm1_gain_grad: float32 [768], replicated
- norm1_bias_grad: float32 [768], replicated
- up_weight_grad: float32 [768, 3072], P('dp', 'tensor')
- up_bias_grad: float32 [3072], P('tensor')
- down_weight_grad: float32 [3072, 768], P('tensor', 'dp')
- down_bias_grad: float32 [768], replicated
- norm2_gain_grad: float32 [768], replicated
- norm2_bias_grad: float32 [768], replicated
- pool_weight_grad: float32 [768, 768], replicated
- pool_bias_grad: float32 [768], replicated
- class_weight_grad: float32 [768, 3], replicated
- class_bias_grad: float32 [3], replicated
Inputs may be any that keep to these rules, and one draw needn't show every extreme that they name: `segments`: along each packed row of 512 tokens the ids never fall; a document holds at most half of 512 tokens.
All inputs are finite; a program needn't handle non-finite values.
Results may differ from a plain program's by a relative error of at most 0.017.
The roundings to bfloat16 on the way count: a program that leaves them out, or rounds other values in their place, can miss the bound.
Values may be sent and summed in bfloat16 or wider, within the bound.
A program may use at most 128 MiB of HBM per device.

v0:
```python
from functools import partial
import jax
import jax.numpy as jnp
from jax import lax
from jax.sharding import PartitionSpec as P

HEAD = 64
epsilon = 1e-12
masked_value = -1e30


def norm_forward(values, norm_gain, norm_shift):
    centre = values - jnp.mean(values, axis=-1, keepdims=True)
    inverse = lax.rsqrt(jnp.mean(centre * centre, axis=-1, keepdims=True) + epsilon)
    normed = centre * inverse
    return (normed * norm_gain + norm_shift, normed, inverse)


def norm_backward(grad_out, normed, inverse, norm_gain):
    scaled = grad_out * norm_gain
    grad_in = inverse * (
        scaled
        - jnp.mean(scaled, axis=-1, keepdims=True)
        - normed * jnp.mean(scaled * normed, axis=-1, keepdims=True)
    )
    return (grad_in, jnp.sum(grad_out * normed, axis=0), jnp.sum(grad_out, axis=0))


def split_heads(rows):
    return rows.reshape(rows.shape[0], rows.shape[1] // HEAD, HEAD)


def masked_scores(query_heads, key_heads, segment_row):
    raw_scores = jnp.einsum(
        "qhe,khe->hqk", query_heads, key_heads, preferred_element_type=jnp.float32
    ) * HEAD ** (-0.5)
    allowed = segment_row[:, None] == segment_row[None, :]
    return (jnp.where(allowed[None], raw_scores, masked_value), allowed)


def attend_sequence(block_items):
    query_seq, key_seq, value_seq, segment_row = block_items
    scores, allowed = masked_scores(split_heads(query_seq), split_heads(key_seq), segment_row)
    largest = jnp.max(scores, axis=-1, keepdims=True)
    exponent = jnp.exp(scores - largest)
    row_total = jnp.sum(exponent, axis=-1, keepdims=True)
    soft_low = (exponent / row_total).astype(jnp.bfloat16)
    context = jnp.einsum(
        "hqk,khe->qhe", soft_low, split_heads(value_seq), preferred_element_type=jnp.float32
    )
    context = context.reshape(query_seq.shape).astype(jnp.bfloat16)
    return (context, largest[..., 0] + jnp.log(row_total[..., 0]))


def attend_backward(block_items):
    query_seq, key_seq, value_seq, segment_row, log_total, grad_context = block_items
    query_heads = split_heads(query_seq)
    key_heads = split_heads(key_seq)
    value_heads = split_heads(value_seq)
    grad_heads = split_heads(grad_context)
    scores, allowed = masked_scores(query_heads, key_heads, segment_row)
    soft_probs = jnp.exp(scores - log_total[..., None])
    grad_values = jnp.einsum(
        "hqk,qhe->khe",
        soft_probs.astype(jnp.bfloat16),
        grad_heads,
        preferred_element_type=jnp.float32,
    )
    grad_soft = jnp.einsum(
        "qhe,khe->hqk", grad_heads, value_heads, preferred_element_type=jnp.float32
    )
    grad_scores = soft_probs * (grad_soft - jnp.sum(soft_probs * grad_soft, axis=-1, keepdims=True))
    grad_low = jnp.where(allowed[None], grad_scores, 0.0).astype(jnp.bfloat16)
    score_scale = HEAD ** (-0.5)
    grad_queries = (
        jnp.einsum("hqk,khe->qhe", grad_low, key_heads, preferred_element_type=jnp.float32)
        * score_scale
    )
    grad_keys = (
        jnp.einsum("hqk,qhe->khe", grad_low, query_heads, preferred_element_type=jnp.float32)
        * score_scale
    )
    full_shape = query_seq.shape
    return (
        grad_queries.reshape(full_shape).astype(jnp.bfloat16),
        grad_keys.reshape(full_shape).astype(jnp.bfloat16),
        grad_values.reshape(full_shape).astype(jnp.bfloat16),
    )


def body(
    inputs,
    segments,
    labels,
    qkv_weight,
    qv_bias,
    out_weight,
    out_bias,
    norm1_gain,
    norm1_bias,
    up_weight,
    up_bias,
    down_weight,
    down_bias,
    norm2_gain,
    norm2_bias,
    pool_weight,
    pool_bias,
    class_weight,
    class_bias,
    cotangent,
):
    share_rows = inputs.shape[0]
    seq_count, seq_length = segments.shape
    offset = lax.axis_index("tensor") * share_rows

    def take_share(array):
        return lax.dynamic_slice_in_dim(array, offset, share_rows, 0)

    gathered = lax.all_gather(inputs, "tensor", axis=0, tiled=True)
    group_rows = gathered.shape[0]
    projected = jnp.einsum("td,kde->kte", gathered, qkv_weight, preferred_element_type=jnp.float32)
    queries = (projected[0] + qv_bias[0]).astype(jnp.bfloat16)
    key_rows = projected[1].astype(jnp.bfloat16)
    value_rows = (projected[2] + qv_bias[1]).astype(jnp.bfloat16)
    local_width = queries.shape[1]

    def by_sequence(rows):
        return rows.reshape(seq_count, seq_length, rows.shape[-1])

    context, log_totals = lax.map(
        attend_sequence,
        (by_sequence(queries), by_sequence(key_rows), by_sequence(value_rows), segments),
    )
    context = context.reshape(group_rows, local_width)
    attended_all = (
        lax.psum(jnp.dot(context, out_weight, preferred_element_type=jnp.float32), "tensor")
        + out_bias
    )
    first_whole, normed_whole, inverse_whole = norm_forward(
        gathered.astype(jnp.float32) + attended_all, norm1_gain, norm1_bias
    )
    first_all = first_whole.astype(jnp.bfloat16)
    normed_one = take_share(normed_whole)
    inverse_one = take_share(inverse_whole)
    up_pre = jnp.dot(first_all, up_weight, preferred_element_type=jnp.float32) + up_bias
    gelu_exact = partial(jax.nn.gelu, approximate=False)
    active = gelu_exact(up_pre).astype(jnp.bfloat16)
    ffn_all = (
        lax.psum(jnp.dot(active, down_weight, preferred_element_type=jnp.float32), "tensor")
        + down_bias
    )
    final_whole, normed_all, inverse_all = norm_forward(
        first_whole + ffn_all, norm2_gain, norm2_bias
    )
    final_norm = take_share(final_whole)
    normed_two = take_share(normed_all)
    inverse_two = take_share(inverse_all)
    positions = offset + jnp.arange(share_rows, dtype=jnp.int32)
    row_starts = jnp.arange(seq_count, dtype=jnp.int32) * seq_length
    selector = (row_starts[:, None] == positions[None, :]).astype(jnp.float32)
    leading_part = jnp.dot(selector, final_norm, precision=lax.Precision.HIGHEST)
    leading = lax.psum(leading_part, "tensor").astype(jnp.bfloat16)
    pooled = jnp.tanh(jnp.dot(leading, pool_weight, preferred_element_type=jnp.float32) + pool_bias)
    pooled_low = pooled.astype(jnp.bfloat16)
    logits = jnp.dot(pooled_low, class_weight, preferred_element_type=jnp.float32) + class_bias
    chosen = (
        labels[:, None] == jnp.arange(class_weight.shape[1], dtype=jnp.int32)[None, :]
    ).astype(jnp.float32)
    grad_logits = (jax.nn.softmax(logits, axis=-1) - chosen).astype(jnp.bfloat16)
    class_weight_grad = jnp.einsum(
        "rd,rc->dc", pooled_low, grad_logits, preferred_element_type=jnp.float32
    )
    class_bias_grad = jnp.sum(grad_logits.astype(jnp.float32), axis=0)
    grad_pre = (
        jnp.einsum("rc,dc->rd", grad_logits, class_weight, preferred_element_type=jnp.float32)
        * (1.0 - pooled * pooled)
    ).astype(jnp.bfloat16)
    pool_weight_grad = jnp.einsum(
        "rd,re->de", leading, grad_pre, preferred_element_type=jnp.float32
    )
    pool_bias_grad = jnp.sum(grad_pre.astype(jnp.float32), axis=0)
    grad_leading = jnp.einsum(
        "re,de->rd", grad_pre, pool_weight, preferred_element_type=jnp.float32
    )
    grad_final = cotangent.astype(jnp.float32) + jnp.einsum(
        "rt,rd->td", selector, grad_leading, precision=lax.Precision.HIGHEST
    )
    grad_second, norm2_gain_grad, norm2_bias_grad = norm_backward(
        grad_final, normed_two, inverse_two, norm2_gain
    )
    grad_fed = grad_second.astype(jnp.bfloat16)
    down_bias_grad = jnp.sum(grad_fed.astype(jnp.float32), axis=0)
    grad_fed_all = lax.all_gather(grad_fed, "tensor", axis=0, tiled=True)
    down_weight_grad = jnp.einsum(
        "tf,td->fd", active, grad_fed_all, preferred_element_type=jnp.float32
    )
    grad_active = jnp.einsum(
        "td,fd->tf", grad_fed_all, down_weight, preferred_element_type=jnp.float32
    )
    grad_up = jax.vjp(gelu_exact, up_pre)[1](grad_active)[0].astype(jnp.bfloat16)
    up_bias_grad = jnp.sum(grad_up.astype(jnp.float32), axis=0)
    up_weight_grad = jnp.einsum("td,tf->df", first_all, grad_up, preferred_element_type=jnp.float32)
    grad_first = (
        lax.psum_scatter(
            jnp.einsum("tf,df->td", grad_up, up_weight, preferred_element_type=jnp.float32),
            "tensor",
            scatter_dimension=0,
            tiled=True,
        )
        + grad_second
    )
    grad_res, norm1_gain_grad, norm1_bias_grad = norm_backward(
        grad_first, normed_one, inverse_one, norm1_gain
    )
    grad_att = grad_res.astype(jnp.bfloat16)
    out_bias_grad = jnp.sum(grad_att.astype(jnp.float32), axis=0)
    grad_att_all = lax.all_gather(grad_att, "tensor", axis=0, tiled=True)
    out_weight_grad = jnp.einsum(
        "te,td->ed", context, grad_att_all, preferred_element_type=jnp.float32
    )
    grad_context = jnp.einsum(
        "td,ed->te", grad_att_all, out_weight, preferred_element_type=jnp.float32
    ).astype(jnp.bfloat16)
    grad_queries, grad_keys, grad_values = lax.map(
        attend_backward,
        (
            by_sequence(queries),
            by_sequence(key_rows),
            by_sequence(value_rows),
            segments,
            log_totals,
            by_sequence(grad_context),
        ),
    )
    stacked = jnp.stack(
        [
            grad_queries.reshape(group_rows, local_width),
            grad_keys.reshape(group_rows, local_width),
            grad_values.reshape(group_rows, local_width),
        ]
    )
    qkv_weight_grad = jnp.einsum(
        "td,kte->kde", gathered, stacked, preferred_element_type=jnp.float32
    )
    qv_bias_grad = jnp.stack(
        [
            jnp.sum(stacked[0].astype(jnp.float32), axis=0),
            jnp.sum(stacked[2].astype(jnp.float32), axis=0),
        ]
    )
    input_grad = (
        lax.psum_scatter(
            jnp.einsum(
                "kte,kde->td", stacked, qkv_weight, preferred_element_type=jnp.float32
            ).astype(jnp.bfloat16),
            "tensor",
            scatter_dimension=0,
            tiled=True,
        ).astype(jnp.float32)
        + grad_res
    ).astype(jnp.bfloat16)
    qkv_sum, out_sum, up_sum, down_sum = (
        lax.psum_scatter(qkv_weight_grad, "dp", scatter_dimension=1, tiled=True),
        lax.psum_scatter(out_weight_grad, "dp", scatter_dimension=1, tiled=True),
        lax.psum_scatter(up_weight_grad, "dp", scatter_dimension=0, tiled=True),
        lax.psum_scatter(down_weight_grad, "dp", scatter_dimension=1, tiled=True),
    )
    token_grads = lax.psum(
        (
            out_bias_grad,
            norm1_gain_grad,
            norm1_bias_grad,
            down_bias_grad,
            norm2_gain_grad,
            norm2_bias_grad,
        ),
        ("dp", "tensor"),
    )
    group_grads = lax.psum(
        (
            qv_bias_grad,
            up_bias_grad,
            pool_weight_grad,
            pool_bias_grad,
            class_weight_grad,
            class_bias_grad,
        ),
        "dp",
    )
    return (
        final_norm.astype(jnp.bfloat16),
        input_grad,
        qkv_sum,
        group_grads[0],
        out_sum,
        token_grads[0],
        token_grads[1],
        token_grads[2],
        up_sum,
        group_grads[1],
        down_sum,
        token_grads[3],
        token_grads[4],
        token_grads[5],
        group_grads[2],
        group_grads[3],
        group_grads[4],
        group_grads[5],
    )


def solution(mesh):
    placed = (
        P(("dp", "tensor"), None),
        P("dp", None),
        P("dp"),
        P(None, None, "tensor"),
        P(None, "tensor"),
        P("tensor", None),
        P(),
        P(),
        P(),
        P(None, "tensor"),
        P("tensor"),
        P("tensor", None),
        P(),
        P(),
        P(),
        P(),
        P(),
        P(),
        P(),
        P(("dp", "tensor"), None),
    )
    return jax.shard_map(
        body,
        mesh=mesh,
        in_specs=placed,
        out_specs=(
            P(("dp", "tensor"), None),
            P(("dp", "tensor"), None),
            P(None, "dp", "tensor"),
            P(None, "tensor"),
            P("tensor", "dp"),
            P(),
            P(),
            P(),
            P("dp", "tensor"),
            P("tensor"),
            P("tensor", "dp"),
            P(),
            P(),
            P(),
            P(),
            P(),
            P(),
            P(),
        ),
        check_vma=False,
    )
```

profile of v0, /device:TPU:0, one launch (start us, length us, event | category | flops | bytes accessed | tf_op | source)
XLA Modules:
  0.0 1093.7 jit_solution(14431650405853245202)
XLA Ops:
  8.8 53.6 %all-gather.4.cloned.1.call-done = bf16[1536,768]{1,0:T(8,128)(2,1)} async-done(((bf16[384,768]{1,0:T(8,128)(2,1)}), bf16[1536,768]{1,0:T(8,128)(2,1)}) %all-gather.4.cloned.1.call-update) | async-done | bytes 2359312 | tf_op jit(solution)/shard_map/all_gather | solution.py:120
  76.6 12.6 %while.26 = (s32[]{:T(128)}, bf16[3,512,192]{1,2,0:T(8,128)(2,1)S(1)}, f32[3,3,512]{2,1,0:T(4,128)}, bf16[3,512,192]{1,2,0:T(8,128)(2,1)S(1)}, s32[3,512]{1,0:T(...) while((s32[]{:T(128)}, bf16[3,512,192]{1,2,0:T(8,128)(2,1)S(1)}, ...), condition=%wide.region_3.4_spmd, body=%wide.region_0.3_spmd.sunk | while | flops 211122688 | bytes 12902513 | solution.py:131
  94.9 170.5 %all-reduce.6.cloned.1.call-done = f32[1536,768]{1,0:T(8,128)} async-done(((f32[1536,768]{1,0:T(8,128)}), f32[1536,768]{1,0:T(8,128)}) %all-reduce.6.cloned.1.call-update) | async-done | bytes 4718608 | tf_op jit(solution)/shard_map/psum | solution.py:137
  272.2 13.3 %multiply_convert_fusion = (bf16[1536,768]{1,0:T(8,128)(2,1)S(1)}, f32[1536,768]{1,0:T(8,128)}, f32[1536,768]{1,0:T(8,128)}) fusion(f32[768]{0:T(1024)S(1)} %copy-done.40, bf16[768,768]{1,0:T(8,128)(2,1)S(1)} %copy-done, f32[1536,768]{1,0:T(8,128)S(1)} %subtract_multiply_fusion.1, f32[768]{0:T(1024)S(1)} %copy-done.35, f32[768]{0:T(1024)S(1)} %copy-done.22), kind=kOutput, calls=%fused_computation.53 | convolution fusion | flops 1893335040 | bytes 17703936 | tf_op jit(solution)/shard_map/dot_general | solution.py:146
  291.2 171.0 %all-reduce.8.cloned.1.call-done = f32[1536,768]{1,0:T(8,128)} async-done(((f32[1536,768]{1,0:T(8,128)}), f32[1536,768]{1,0:T(8,128)}) %all-reduce.8.cloned.1.call-update) | async-done | bytes 4718608 | tf_op jit(solution)/shard_map/psum | solution.py:150
  470.8 16.4 %psum.107 = bf16[3,768]{1,0:T(4,128)(2,1)S(1)} all-reduce(f32[3,768]{1,0:T(4,128)S(1)} %fusion.56), channel_id=1, replica_groups=mesh['dp'=8,'tensor'=4] {'tensor'}, use_global_device_ids=true, to_apply=%region_10.11 | all-reduce | flops 2304 | bytes 13824 | tf_op jit(solution)/shard_map/psum | solution.py:163
  496.2 47.9 %all-gather.6.cloned.1.call-done = bf16[1536,768]{1,0:T(8,128)(2,1)} async-done(((bf16[384,768]{1,0:T(8,128)(2,1)}), bf16[1536,768]{1,0:T(8,128)(2,1)}) %all-gather.6.cloned.1.call-update) | async-done | bytes 2359312 | tf_op jit(solution)/shard_map/all_gather | solution.py:194
  544.1 8.8 convert_reduce_fusion
  559.5 83.4 %reduce-scatter.11.cloned.1.call-done = f32[384,768]{1,0:T(8,128)} async-done(((f32[1536,768]{1,0:T(8,128)}), f32[384,768]{1,0:T(8,128)}) %reduce-scatter.11.cloned.1.call-update) | async-done | bytes 1179664 | tf_op jit(solution)/shard_map/reduce_scatter | solution.py:205
  651.2 50.4 %all-gather.8.cloned.1.call-done = bf16[1536,768]{1,0:T(8,128)(2,1)} async-done(((bf16[384,768]{1,0:T(8,128)(2,1)}), bf16[1536,768]{1,0:T(8,128)(2,1)}) %all-gather.8.cloned.1.call-update) | async-done | bytes 2359312 | tf_op jit(solution)/shard_map/all_gather | solution.py:218
  706.1 75.7 %while.27 = (s32[]{:T(128)}, bf16[3,512,192]{1,2,0:T(8,128)(2,1)S(1)}, bf16[3,512,192]{1,2,0:T(8,128)(2,1)}, bf16[3,512,192]{1,2,0:T(8,128)(2,1)S(1)}, bf16[3,51...) while((s32[]{:T(128)}, ...), condition=%wide.region_20.21_spmd, body=%wide.region_18.20_spmd.sunk | while | flops 515084288 | bytes 27811988 | solution.py:225
  724.8 5.8 fusion.178
  741.7 5.8 fusion.176
  750.0 5.8 fusion.178
  767.0 5.8 fusion.176
  775.3 5.8 fusion.178
  821.7 6.6 fusion.58
  828.5 5.9 fusion.96
  836.0 40.0 %all-reduce = (f32[768]{0:T(1024)}, f32[768]{0:T(1024)}, f32[768]{0:T(1024)}, f32[768]{0:T(1024)}, f32[768]{0:T(1024)}, /*index=5*/f32[768]{0:T(1024)}) all-reduce(f32[768]{0:T(1024)} %get-tuple-element.275, f32[768]{0:T(1024)} %get-tuple-element.222, ...), channel_id=1, replica_groups=mesh['dp'=8,'tensor'=4] {'dp','tensor'}, use_global_device_ids=true, to_apply=%region_28.29 | all-reduce | flops 4608 | bytes 36864 | tf_op jit(solution)/shard_map/psum | solution.py:269
  876.3 25.2 %all-reduce.1 = (f32[2,192]{1,0:T(2,128)}, f32[768]{0:T(1024)}, f32[768]{0:T(1024)}, f32[768,3]{0,1:T(4,128)}, f32[3]{0:T(128)}) all-reduce(f32[2,192]{1,0:T(2,128)S(1)} %pad_maximum_fusion, f32[768]{0:T(1024)} %get-tuple-element.279, f32[768]{0:T(1024)} %get-tuple-element.301, ...), channel_id=1, replica_groups=mesh['dp'=8,'tensor'=4] {'dp'}, use_global_device_ids=true, to_apply=%region_25.26 | all-reduce | flops 4227 | bytes 33816 | tf_op jit(solution)/shard_map/psum | solution.py:280
  905.0 21.0 %reduce-scatter.13.cloned.1.call-done = bf16[384,768]{1,0:T(8,128)(2,1)} async-done(((bf16[1536,768]{1,0:T(8,128)(2,1)}), bf16[384,768]{1,0:T(8,128)(2,1)}) %reduce-scatter.13.cloned.1.call-update) | async-done | bytes 589840 | tf_op jit(solution)/shard_map/reduce_scatter | solution.py:253
  928.7 62.9 %all-reduce.10.cloned.1.call-done = f32[768,768]{1,0:T(8,128)} async-done(((f32[768,768]{1,0:T(8,128)}), f32[768,768]{1,0:T(8,128)}) %all-reduce.10.cloned.1.call-update) | async-done | bytes 2359312 | tf_op jit(solution)/shard_map/psum | solution.py:280
  991.6 45.7 %reduce-scatter.15.cloned.1.call-done = f32[96,768]{1,0:T(8,128)} async-done(((f32[768,768]{1,0:T(8,128)}), f32[96,768]{1,0:T(8,128)}) %reduce-scatter.15.cloned.1.call-update) | async-done | bytes 294928 | tf_op jit(solution)/shard_map/reduce_scatter | solution.py:266
  1037.2 46.2 %reduce-scatter.17.cloned.1.call-done = f32[768,96]{0,1:T(8,128)} async-done(((f32[768,768]{0,1:T(8,128)}), f32[768,96]{0,1:T(8,128)}) %reduce-scatter.17.cloned.1.call-update) | async-done | bytes 294928 | tf_op jit(solution)/shard_map/reduce_scatter | solution.py:267
  (255 shorter events, 180.7 us)
Async XLA Ops:
  7.2 265.0 %copy-start = (bf16[768,768]{1,0:T(8,128)(2,1)S(1)}, bf16[768,768]{1,0:T(8,128)(2,1)}, u32[]{:S(2)}) copy-start(bf16[768,768]{1,0:T(8,128)(2,1)} %param.33) | copy-start | bytes 3538948
  7.2 55.1 %all-gather.4.cloned.1.call-start = ((), (), s32[]{:S(2)}) async-start(), calls=%async_computation.6 | async-start | bytes 2949120 | tf_op jit(solution)/shard_map/all_gather | solution.py:120
  7.9 257.5 %all-reduce.6.cloned.1.call-start = ((), (), s32[]{:S(2)}) async-start(), calls=%async_computation.7 | async-start | bytes 9437184 | tf_op jit(solution)/shard_map/psum | solution.py:137
  94.5 170.9 %copy-start.3 = (bf16[1536,768]{1,0:T(8,128)(2,1)S(1)}, bf16[1536,768]{1,0:T(8,128)(2,1)}, u32[]{:S(2)}) copy-start(bf16[1536,768]{1,0:T(8,128)(2,1)} %all-gather.4.cloned.1.call-done) | copy-start | bytes 7077892
  94.5 170.9 %copy-start.26 = (f32[768]{0:T(1024)S(1)}, f32[768]{0:T(1024)}, u32[]{:S(2)}) copy-start(f32[768]{0:T(1024)} %param.30) | copy-start | bytes 9220
  94.5 367.7 %all-reduce.8.cloned.1.call-start = ((), (), s32[]{:S(2)}) async-start(), calls=%async_computation.8 | async-start | bytes 9437184 | tf_op jit(solution)/shard_map/psum | solution.py:150
  291.1 171.1 %copy-start.33 = (f32[768]{0:T(1024)S(1)}, f32[768]{0:T(1024)}, u32[]{:S(2)}) copy-start(f32[768]{0:T(1024)} %param.36) | copy-start | bytes 9220
  291.1 253.0 %all-gather.6.cloned.1.call-start = ((), (), s32[]{:S(2)}) async-start(), calls=%async_computation.9 | async-start | bytes 2949120 | tf_op jit(solution)/shard_map/all_gather | solution.py:194
  489.6 54.5 %copy-start.41 = (f32[768]{0:T(1024)S(1)}, f32[768]{0:T(1024)}, u32[]{:S(2)}) copy-start(f32[768]{0:T(1024)} %param.34) | copy-start | bytes 9220
  495.6 147.2 %reduce-scatter.11.cloned.1.call-start = ((), (), s32[]{:S(2)}) async-start(), calls=%async_computation.10 | async-start | bytes 5898240 | tf_op jit(solution)/shard_map/reduce_scatter | solution.py:205
  558.6 143.0 %all-gather.8.cloned.1.call-start = ((), (), s32[]{:S(2)}) async-start(), calls=%async_computation.11 | async-start | bytes 2949120 | tf_op jit(solution)/shard_map/all_gather | solution.py:218
  559.4 87.5 %copy-start.29 = (f32[384]{0:T(512)}, f32[384]{0:T(512)S(1)}, u32[]{:S(2)}) copy-start(f32[384]{0:T(512)S(1)} %dynamic-slice.6) | copy-start | bytes 4612
  646.9 54.7 %copy-start.19 = (bf16[192,768]{1,0:T(8,128)(2,1)S(1)}, bf16[192,768]{1,0:T(8,128)(2,1)}, u32[]{:S(2)}) copy-start(bf16[192,768]{1,0:T(8,128)(2,1)} %param.29) | copy-start | bytes 884740
  647.0 57.3 %copy-start.30 = (f32[384]{0:T(512)}, f32[384]{0:T(512)S(1)}, u32[]{:S(2)}) copy-start(f32[384]{0:T(512)S(1)} %broadcast_multiply_fusion.2) | copy-start | bytes 4612
  647.0 57.3 %copy-start.31 = (f32[384]{0:T(512)}, f32[384]{0:T(512)S(1)}, u32[]{:S(2)}) copy-start(f32[384]{0:T(512)S(1)} %broadcast_multiply_fusion.3) | copy-start | bytes 4612
  651.0 250.5 %reduce-scatter.21.cloned.1.call-start = ((), (), s32[]{:S(2)}) async-start(), calls=%async_computation.17 | async-start | bytes 884736
  797.5 105.6 %reduce-scatter.19.cloned.1.call-start = ((), (), s32[]{:S(2)}) async-start(), calls=%async_computation.16 | async-start | bytes 2211840
  814.7 111.3 %reduce-scatter.13.cloned.1.call-start = ((), (), s32[]{:S(2)}) async-start(), calls=%async_computation.12 | async-start | bytes 2949120 | tf_op jit(solution)/shard_map/reduce_scatter | solution.py:253
  819.6 171.9 %all-reduce.10.cloned.1.call-start = ((), (), s32[]{:S(2)}) async-start(), calls=%async_computation.15 | async-start | bytes 4718592 | tf_op jit(solution)/shard_map/psum | solution.py:280
  821.7 215.5 %reduce-scatter.15.cloned.1.call-start = ((), (), s32[]{:S(2)}) async-start(), calls=%async_computation.13 | async-start | bytes 2654208 | tf_op jit(solution)/shard_map/reduce_scatter | solution.py:266
  828.4 47.6 %copy-start.14 = (bf16[3,512,192]{1,2,0:T(8,128)(2,1)S(1)}, bf16[3,512,192]{1,2,0:T(8,128)(2,1)}, u32[]{:S(2)}) copy-start(bf16[3,512,192]{1,2,0:T(8,128)(2,1)} %copy-done.13) | copy-start | bytes 1769476
  828.4 254.9 %reduce-scatter.17.cloned.1.call-start = ((), (), s32[]{:S(2)}) async-start(), calls=%async_computation.14 | async-start | bytes 2654208 | tf_op jit(solution)/shard_map/reduce_scatter | solution.py:267
  834.4 41.7 %copy-start.12 = (bf16[3,512,192]{1,2,0:T(8,128)(2,1)S(1)}, bf16[3,512,192]{1,2,0:T(8,128)(2,1)}, u32[]{:S(2)}) copy-start(bf16[3,512,192]{1,2,0:T(8,128)(2,1)} %copy-done.11) | copy-start | bytes 1769476
  834.4 91.7 %copy-start.10 = (f32[384,768]{1,0:T(8,128)S(1)}, f32[384,768]{1,0:T(8,128)}, u32[]{:S(2)}) copy-start(f32[384,768]{1,0:T(8,128)} %copy-done.9) | copy-start | bytes 3538948
  (33 other events, 230.6 us)
Sparse Core Ops, SparseCore 0:
  9.6 52.6 all-gather.3
  94.7 170.7 all-reduce.5
  291.2 170.9 all-reduce.7
  495.7 48.3 all-gather.5
  558.7 84.0 reduce-scatter.10
  651.1 50.4 all-gather.7
  797.7 33.6 reduce-scatter.20
  834.8 40.5 reduce-scatter.18
  878.3 47.6 reduce-scatter.12
  929.2 62.3 all-reduce.9
  995.5 41.6 reduce-scatter.14
  1041.0 42.3 reduce-scatter.16
where the time goes:
time: 1100 us; the launch traced here: 1090 us
  waiting for transfers between devices  753 us (68%)
  matrix products  137 us (12%)
  blocking collectives  81.6 us (7%)
  local copies, waits for them, and re-layouts  73.4 us (7%)
  other arithmetic  31 us (3%)
  between operations  15 us (1%)
    psum x1, waiting for transfers between devices, body(): lax.psum(jnp.dot(active, down_weight, preferred_element_type=jnp.float32)...  171 us
    psum x1, waiting for transfers between devices, body(): lax.psum(jnp.dot(context, out_weight, preferred_element_type=jnp.float32)...  171 us
    reduce_scatter x1, waiting for transfers between devices, body(): lax.psum_scatter(jnp.einsum('tf,df->td', grad_up, up_weight, preferred_el...  83.4 us
    psum x1, waiting for transfers between devices, body(): lax.psum((qv_bias_grad, up_bias_grad, pool_weight_grad, pool_bias_grad, c...  62.9 us
    all_gather x1, waiting for transfers between devices, body(): gathered = lax.all_gather(inputs, 'tensor', axis=0, tiled=True)  53.6 us
    all_gather x1, waiting for transfers between devices, body(): grad_att_all = lax.all_gather(grad_att, 'tensor', axis=0, tiled=True)  50.4 us
    all_gather x1, waiting for transfers between devices, body(): grad_fed_all = lax.all_gather(grad_fed, 'tensor', axis=0, tiled=True)  47.9 us
    reduce_scatter x1, waiting for transfers between devices, body(): lax.psum_scatter(down_weight_grad, 'dp', scatter_dimension=1, tiled=True)  46.2 us
  transfers between devices with their start and end apart: 12, of which 10 were waited for; matrix products, arithmetic and copies ran while one was open for 4% of the time, Pallas kernels for 0%

commit v1 on v0

--- a/solution.py
+++ b/solution.py
@@ -147,7 +147,12 @@
     gelu_exact = partial(jax.nn.gelu, approximate=False)
     active = gelu_exact(up_pre).astype(jnp.bfloat16)
     ffn_all = (
-        lax.psum(jnp.dot(active, down_weight, preferred_element_type=jnp.float32), "tensor")
+        jnp.sum(
+            lax.all_gather(
+                jnp.dot(active, down_weight, preferred_element_type=jnp.float32), "tensor"
+            ),
+            axis=0,
+        )
         + down_bias
     )
     final_whole, normed_all, inverse_all = norm_forward(

time: 1100 us -> 1260 us (1.15)
  waiting for transfers between devices: 753 us -> 904 us
    all_gather x0 -> x1, waiting for transfers between devices: none -> 322 us  [body(): lax.all_gather(jnp.dot(active, down_weight, preferred_element_type=jnp.fl...]
    psum x1 -> x0, waiting for transfers between devices: 171 us -> none  [body(): lax.psum(jnp.dot(active, down_weight, preferred_element_type=jnp.float32)...]
where the time goes in v1:
time: 1260 us; the launch traced here: 1250 us
  waiting for transfers between devices  904 us (72%)
  matrix products  136 us (11%)
  blocking collectives  81.9 us (7%)
  local copies, waits for them, and re-layouts  73.5 us (6%)
  other arithmetic  41.4 us (3%)
  between operations  15 us (1%)
    all_gather x1, waiting for transfers between devices, body(): lax.all_gather(jnp.dot(active, down_weight, preferred_element_type=jnp.fl...  322 us
    psum x1, waiting for transfers between devices, body(): lax.psum(jnp.dot(context, out_weight, preferred_element_type=jnp.float32)...  171 us
    reduce_scatter x1, waiting for transfers between devices, body(): lax.psum_scatter(jnp.einsum('tf,df->td', grad_up, up_weight, preferred_el...  83.4 us
    psum x1, waiting for transfers between devices, body(): lax.psum((qv_bias_grad, up_bias_grad, pool_weight_grad, pool_bias_grad, c...  62.9 us
    all_gather x1, waiting for transfers between devices, body(): gathered = lax.all_gather(inputs, 'tensor', axis=0, tiled=True)  53.6 us
    all_gather x1, waiting for transfers between devices, body(): grad_att_all = lax.all_gather(grad_att, 'tensor', axis=0, tiled=True)  50.2 us
    all_gather x1, waiting for transfers between devices, body(): grad_fed_all = lax.all_gather(grad_fed, 'tensor', axis=0, tiled=True)  48.4 us
    reduce_scatter x1, waiting for transfers between devices, body(): lax.psum_scatter(up_weight_grad, 'dp', scatter_dimension=0, tiled=True)  46.2 us
  transfers between devices with their start and end apart: 12, of which 10 were waited for; matrix products, arithmetic and copies ran while one was open for 4% of the time, Pallas kernels for 0%

profile of v1, /device:TPU:0, one launch (start us, length us, event | category | flops | bytes accessed | tf_op | source)
XLA Modules:
  0.0 1254.1 jit_solution(7867066773307021685)
XLA Ops:
  8.8 53.6 %all-gather.6.cloned.1.call-done = bf16[1536,768]{1,0:T(8,128)(2,1)} async-done(((bf16[384,768]{1,0:T(8,128)(2,1)}), bf16[1536,768]{1,0:T(8,128)(2,1)}) %all-gather.6.cloned.1.call-update) | async-done | bytes 2359312 | tf_op jit(solution)/shard_map/all_gather | solution.py:120
  76.6 12.6 %while.26 = (s32[]{:T(128)}, bf16[3,512,192]{1,2,0:T(8,128)(2,1)S(1)}, f32[3,3,512]{2,1,0:T(4,128)}, bf16[3,512,192]{1,2,0:T(8,128)(2,1)S(1)}, s32[3,512]{1,0:T(...) while((s32[]{:T(128)}, bf16[3,512,192]{1,2,0:T(8,128)(2,1)S(1)}, ...), condition=%wide.region_3.4_spmd, body=%wide.region_0.3_spmd.sunk | while | flops 211122688 | bytes 12903013 | solution.py:131
  94.8 170.7 %all-reduce.5.cloned.1.call-done = f32[1536,768]{1,0:T(8,128)} async-done(((f32[1536,768]{1,0:T(8,128)}), f32[1536,768]{1,0:T(8,128)}) %all-reduce.5.cloned.1.call-update) | async-done | bytes 4718608 | tf_op jit(solution)/shard_map/psum | solution.py:137
  272.2 13.2 %multiply_convert_fusion = (bf16[1536,768]{1,0:T(8,128)(2,1)S(1)}, f32[1536,768]{1,0:T(8,128)}, f32[1536,768]{1,0:T(8,128)}) fusion(f32[768]{0:T(1024)S(1)} %copy-done.41, bf16[768,768]{1,0:T(8,128)(2,1)S(1)} %copy-done, f32[1536,768]{1,0:T(8,128)S(1)} %subtract_multiply_fusion.1, f32[768]{0:T(1024)S(1)} %copy-done.35, f32[768]{0:T(1024)S(1)} %copy-done.22), kind=kOutput, calls=%fused_computation.53 | convolution fusion | flops 1893335040 | bytes 17703936 | tf_op jit(solution)/shard_map/dot_general | solution.py:146
  291.2 321.6 %all-gather.12.cloned.1.call-done = f32[6144,768]{1,0:T(8,128)} async-done(((f32[1536,768]{1,0:T(8,128)}), f32[6144,768]{1,0:T(8,128)}) %all-gather.12.cloned.1.call-update) | async-done | bytes 18874384 | tf_op jit(solution)/shard_map/all_gather | solution.py:151
  612.8 10.4 reduce_sum.209
  631.9 16.6 %psum.99 = bf16[3,768]{1,0:T(4,128)(2,1)S(1)} all-reduce(f32[3,768]{1,0:T(4,128)S(1)} %fusion.56), channel_id=1, replica_groups=mesh['dp'=8,'tensor'=4] {'tensor'}, use_global_device_ids=true, to_apply=%region_10.11 | all-reduce | flops 2304 | bytes 13824 | tf_op jit(solution)/shard_map/psum | solution.py:168
  656.9 48.4 %all-gather.8.cloned.1.call-done = bf16[1536,768]{1,0:T(8,128)(2,1)} async-done(((bf16[384,768]{1,0:T(8,128)(2,1)}), bf16[1536,768]{1,0:T(8,128)(2,1)}) %all-gather.8.cloned.1.call-update) | async-done | bytes 2359312 | tf_op jit(solution)/shard_map/all_gather | solution.py:199
  705.4 8.8 convert_reduce_fusion
  720.7 83.4 %reduce-scatter.11.cloned.1.call-done = f32[384,768]{1,0:T(8,128)} async-done(((f32[1536,768]{1,0:T(8,128)}), f32[384,768]{1,0:T(8,128)}) %reduce-scatter.11.cloned.1.call-update) | async-done | bytes 1179664 | tf_op jit(solution)/shard_map/reduce_scatter | solution.py:210
  812.7 50.2 %all-gather.10.cloned.1.call-done = bf16[1536,768]{1,0:T(8,128)(2,1)} async-done(((bf16[384,768]{1,0:T(8,128)(2,1)}), bf16[1536,768]{1,0:T(8,128)(2,1)}) %all-gather.10.cloned.1.call-update) | async-done | bytes 2359312 | tf_op jit(solution)/shard_map/all_gather | solution.py:223
  867.4 74.8 %while.27 = (s32[]{:T(128)}, bf16[3,512,192]{1,2,0:T(8,128)(2,1)S(1)}, bf16[3,512,192]{1,2,0:T(8,128)(2,1)}, bf16[3,512,192]{1,2,0:T(8,128)(2,1)S(1)}, bf16[3,51...) while((s32[]{:T(128)}, ...), condition=%wide.region_20.21_spmd, body=%wide.region_18.20_spmd.sunk | while | flops 515084288 | bytes 27812488 | solution.py:230
  877.8 5.7 fusion.178
  902.7 5.7 fusion.178
  927.6 5.7 fusion.178
  936.5 5.6 fusion.176
  982.1 5.9 fusion.96
  988.1 6.7 fusion.58
  996.4 40.1 %all-reduce = (f32[768]{0:T(1024)}, f32[768]{0:T(1024)}, f32[768]{0:T(1024)}, f32[768]{0:T(1024)}, f32[768]{0:T(1024)}, /*index=5*/f32[768]{0:T(1024)}) all-reduce(f32[768]{0:T(1024)} %get-tuple-element.275, f32[768]{0:T(1024)} %get-tuple-element.222, ...), channel_id=1, replica_groups=mesh['dp'=8,'tensor'=4] {'dp','tensor'}, use_global_device_ids=true, to_apply=%region_28.29 | all-reduce | flops 4608 | bytes 36864 | tf_op jit(solution)/shard_map/psum | solution.py:274
  1036.8 25.2 %all-reduce.1 = (f32[2,192]{1,0:T(2,128)}, f32[768]{0:T(1024)}, f32[768]{0:T(1024)}, f32[768,3]{0,1:T(4,128)}, f32[3]{0:T(128)}) all-reduce(f32[2,192]{1,0:T(2,128)S(1)} %pad_maximum_fusion, f32[768]{0:T(1024)} %get-tuple-element.279, f32[768]{0:T(1024)} %get-tuple-element.301, ...), channel_id=1, replica_groups=mesh['dp'=8,'tensor'=4] {'dp'}, use_global_device_ids=true, to_apply=%region_25.26 | all-reduce | flops 4227 | bytes 33816 | tf_op jit(solution)/shard_map/psum | solution.py:285
  1065.5 21.0 %reduce-scatter.13.cloned.1.call-done = bf16[384,768]{1,0:T(8,128)(2,1)} async-done(((bf16[1536,768]{1,0:T(8,128)(2,1)}), bf16[384,768]{1,0:T(8,128)(2,1)}) %reduce-scatter.13.cloned.1.call-update) | async-done | bytes 589840 | tf_op jit(solution)/shard_map/reduce_scatter | solution.py:258
  1089.1 62.9 %all-reduce.7.cloned.1.call-done = f32[768,768]{1,0:T(8,128)} async-done(((f32[768,768]{1,0:T(8,128)}), f32[768,768]{1,0:T(8,128)}) %all-reduce.7.cloned.1.call-update) | async-done | bytes 2359312 | tf_op jit(solution)/shard_map/psum | solution.py:285
  1152.0 45.7 %reduce-scatter.17.cloned.1.call-done = f32[768,96]{0,1:T(8,128)} async-done(((f32[768,768]{0,1:T(8,128)}), f32[768,96]{0,1:T(8,128)}) %reduce-scatter.17.cloned.1.call-update) | async-done | bytes 294928 | tf_op jit(solution)/shard_map/reduce_scatter | solution.py:272
  1197.7 46.2 %reduce-scatter.15.cloned.1.call-done = f32[96,768]{1,0:T(8,128)} async-done(((f32[768,768]{1,0:T(8,128)}), f32[96,768]{1,0:T(8,128)}) %reduce-scatter.15.cloned.1.call-update) | async-done | bytes 294928 | tf_op jit(solution)/shard_map/reduce_scatter | solution.py:271
  (256 shorter events, 185.7 us)
Async XLA Ops:
  7.2 265.0 %copy-start = (bf16[768,768]{1,0:T(8,128)(2,1)S(1)}, bf16[768,768]{1,0:T(8,128)(2,1)}, u32[]{:S(2)}) copy-start(bf16[768,768]{1,0:T(8,128)(2,1)} %param.33) | copy-start | bytes 3538948
  7.2 55.1 %all-gather.6.cloned.1.call-start = ((), (), s32[]{:S(2)}) async-start(), calls=%async_computation.6 | async-start | bytes 2949120 | tf_op jit(solution)/shard_map/all_gather | solution.py:120
  7.9 257.5 %all-reduce.5.cloned.1.call-start = ((), (), s32[]{:S(2)}) async-start(), calls=%async_computation.7 | async-start | bytes 9437184 | tf_op jit(solution)/shard_map/psum | solution.py:137
  94.5 170.9 %copy-start.3 = (bf16[1536,768]{1,0:T(8,128)(2,1)S(1)}, bf16[1536,768]{1,0:T(8,128)(2,1)}, u32[]{:S(2)}) copy-start(bf16[1536,768]{1,0:T(8,128)(2,1)} %all-gather.6.cloned.1.call-done) | copy-start | bytes 7077892
  94.5 170.9 %copy-start.26 = (f32[768]{0:T(1024)S(1)}, f32[768]{0:T(1024)}, u32[]{:S(2)}) copy-start(f32[768]{0:T(1024)} %param.30) | copy-start | bytes 9220
  94.6 518.3 %all-gather.12.cloned.1.call-start = ((), (), s32[]{:S(2)}) async-start(), calls=%async_computation.15 | async-start | bytes 23592960 | tf_op jit(solution)/shard_map/all_gather | solution.py:151
  291.1 414.2 %all-gather.8.cloned.1.call-start = ((), (), s32[]{:S(2)}) async-start(), calls=%async_computation.8 | async-start | bytes 2949120 | tf_op jit(solution)/shard_map/all_gather | solution.py:199
  628.7 20.3 %copy-start.38 = (s32[3]{0:T(128)S(1)}, s32[3]{0:T(128)}, u32[]{:S(2)}) copy-start(s32[3]{0:T(128)} %param.26) | copy-start | bytes 40
  629.2 21.6 %copy-start.18 = (bf16[384,768]{1,0:T(8,128)(2,1)S(1)}, bf16[384,768]{1,0:T(8,128)(2,1)}, u32[]{:S(2)}) copy-start(bf16[384,768]{1,0:T(8,128)(2,1)} %param.43) | copy-start | bytes 1769476
  656.9 147.2 %reduce-scatter.11.cloned.1.call-start = ((), (), s32[]{:S(2)}) async-start(), calls=%async_computation.9 | async-start | bytes 5898240 | tf_op jit(solution)/shard_map/reduce_scatter | solution.py:210
  719.9 143.0 %all-gather.10.cloned.1.call-start = ((), (), s32[]{:S(2)}) async-start(), calls=%async_computation.10 | async-start | bytes 2949120 | tf_op jit(solution)/shard_map/all_gather | solution.py:223
  720.7 87.5 %copy-start.29 = (f32[384]{0:T(512)}, f32[384]{0:T(512)S(1)}, u32[]{:S(2)}) copy-start(f32[384]{0:T(512)S(1)} %dynamic-slice.6) | copy-start | bytes 4612
  808.2 54.7 %copy-start.19 = (bf16[192,768]{1,0:T(8,128)(2,1)S(1)}, bf16[192,768]{1,0:T(8,128)(2,1)}, u32[]{:S(2)}) copy-start(bf16[192,768]{1,0:T(8,128)(2,1)} %param.29) | copy-start | bytes 884740
  808.2 57.3 %copy-start.30 = (f32[384]{0:T(512)}, f32[384]{0:T(512)S(1)}, u32[]{:S(2)}) copy-start(f32[384]{0:T(512)S(1)} %broadcast_multiply_fusion.2) | copy-start | bytes 4612
  808.2 57.3 %copy-start.31 = (f32[384]{0:T(512)}, f32[384]{0:T(512)S(1)}, u32[]{:S(2)}) copy-start(f32[384]{0:T(512)S(1)} %broadcast_multiply_fusion.3) | copy-start | bytes 4612
  812.3 249.7 %reduce-scatter.21.cloned.1.call-start = ((), (), s32[]{:S(2)}) async-start(), calls=%async_computation.17 | async-start | bytes 884736
  957.9 105.7 %reduce-scatter.19.cloned.1.call-start = ((), (), s32[]{:S(2)}) async-start(), calls=%async_computation.16 | async-start | bytes 2211840
  975.1 111.4 %reduce-scatter.13.cloned.1.call-start = ((), (), s32[]{:S(2)}) async-start(), calls=%async_computation.11 | async-start | bytes 2949120 | tf_op jit(solution)/shard_map/reduce_scatter | solution.py:258
  980.0 172.0 %all-reduce.7.cloned.1.call-start = ((), (), s32[]{:S(2)}) async-start(), calls=%async_computation.14 | async-start | bytes 4718592 | tf_op jit(solution)/shard_map/psum | solution.py:285
  982.1 215.6 %reduce-scatter.17.cloned.1.call-start = ((), (), s32[]{:S(2)}) async-start(), calls=%async_computation.13 | async-start | bytes 2654208 | tf_op jit(solution)/shard_map/reduce_scatter | solution.py:272
  988.0 48.5 %copy-start.12 = (bf16[3,512,192]{1,2,0:T(8,128)(2,1)S(1)}, bf16[3,512,192]{1,2,0:T(8,128)(2,1)}, u32[]{:S(2)}) copy-start(bf16[3,512,192]{1,2,0:T(8,128)(2,1)} %copy-done.11) | copy-start | bytes 1769476
  988.0 255.8 %reduce-scatter.15.cloned.1.call-start = ((), (), s32[]{:S(2)}) async-start(), calls=%async_computation.12 | async-start | bytes 2654208 | tf_op jit(solution)/shard_map/reduce_scatter | solution.py:271
  994.8 41.8 %copy-start.14 = (bf16[3,512,192]{1,2,0:T(8,128)(2,1)S(1)}, bf16[3,512,192]{1,2,0:T(8,128)(2,1)}, u32[]{:S(2)}) copy-start(bf16[3,512,192]{1,2,0:T(8,128)(2,1)} %copy-done.13) | copy-start | bytes 1769476
  994.8 91.7 %copy-start.10 = (f32[384,768]{1,0:T(8,128)S(1)}, f32[384,768]{1,0:T(8,128)}, u32[]{:S(2)}) copy-start(f32[384,768]{1,0:T(8,128)} %copy-done.9) | copy-start | bytes 3538948
  (33 other events, 207.0 us)
Sparse Core Ops, SparseCore 0:
  9.6 52.6 all-gather.5
  94.7 170.7 all-reduce.4
  291.3 321.5 all-gather.11
  657.0 48.3 all-gather.7
  720.0 84.0 reduce-scatter.10
  812.4 50.4 all-gather.9
  958.0 33.6 reduce-scatter.20
  995.2 40.5 reduce-scatter.18
  1038.7 47.7 reduce-scatter.12
  1089.6 62.3 all-reduce.6
  1155.9 41.6 reduce-scatter.16
  1201.4 42.3 reduce-scatter.14
